TPU v7x, 32 devices: a whole 2x2x4 slice. The times are simulated.
32 devices in a mesh: group: 16 (over z, y, core), shard: 2 (over x).
Axes of the slice: x: 2, y: 2, z: 4, core: 2. Of those that a mesh axis runs over, the one named last changes fastest.
Arguments:
- tokens: float32 [16384, 1024], P(('group', 'shard')), may hold values from -6 to 6
- cotangent: float32 [16384, 1024], P(('group', 'shard')), may hold values from -6 to 6
- lengths: int32 [16], replicated, may hold values from 512 to 1024, as said below
- qkv_weight: float32 [1024, 3072], P('shard'), may hold values from -0.1875 to 0.1875
- qkv_momentum: float32 [1024, 3072], P('shard')
- qkv_average: float32 [1024, 3072], P('shard'), may hold values from -0.1875 to 0.1875
- out_weight: float32 [1024, 1024], P('shard'), may hold values from -0.5 to 0.5
- out_momentum: float32 [1024, 1024], P('shard')
- out_average: float32 [1024, 1024], P('shard'), may hold values from -0.5 to 0.5
- up_weight: float32 [1024, 4096], P(None, 'shard'), may hold values from -0.1875 to 0.1875
- up_momentum: float32 [1024, 4096], P(None, 'shard')
- up_average: float32 [1024, 4096], P(None, 'shard'), may hold values from -0.1875 to 0.1875
- down_weight: float32 [4096, 1024], P('shard'), may hold values from -0.09375 to 0.09375
- down_momentum: float32 [4096, 1024], P('shard')
- down_average: float32 [4096, 1024], P('shard'), may hold values from -0.09375 to 0.09375
- small_params: float32 [12, 1024], P(None, 'shard')
- small_momentum: float32 [12, 1024], P(None, 'shard')
- small_average: float32 [12, 1024], P(None, 'shard')
Outputs:
- block_out: float32 [16384, 1024], P(('group', 'shard'))
- input_grad: float32 [16384, 1024], P(('group', 'shard'))
- qkv_weight_new: float32 [1024, 3072], P('shard')
- qkv_momentum_new: float32 [1024, 3072], P('shard')
- qkv_average_new: float32 [1024, 3072], P('shard')
- out_weight_new: float32 [1024, 1024], P('shard')
- out_momentum_new: float32 [1024, 1024], P('shard')
- out_average_new: float32 [1024, 1024], P('shard')
- up_weight_new: float32 [1024, 4096], P(None, 'shard')
- up_momentum_new: float32 [1024, 4096], P(None, 'shard')
- up_average_new: float32 [1024, 4096], P(None, 'shard')
- down_weight_new: float32 [4096, 1024], P('shard')
- down_momentum_new: float32 [4096, 1024], P('shard')
- down_average_new: float32 [4096, 1024], P('shard')
- small_params_new: float32 [12, 1024], P(None, 'shard')
- small_momentum_new: float32 [12, 1024], P(None, 'shard')
- small_average_new: float32 [12, 1024], P(None, 'shard')
Inputs may be any that keep to these rules, and one draw needn't show every extreme that they name: `lengths`: the first 512 positions of every sequence are live; in every draw some sequence is live in all 1024 positions and some in exactly 512.
All inputs are finite; a program needn't handle non-finite values.
Results may differ from a plain program's by a relative error of at most 0.012.
Values may be sent and summed in bfloat16 or wider, within the bound.
A program may use at most 384 MiB of HBM per device.

v0:
```python
import functools
import math

import jax
import jax.numpy as jnp
from jax import lax
from jax.experimental import pallas as pl
from jax.experimental.pallas import tpu as pltpu
from jax.sharding import PartitionSpec as P


HEADS = 16
FF = 4096


EPS = 1e-05
MOMENTUM = 0.9
AVERAGING = 0.9
NEG_FILL = -1e30
SHARD = "shard"
OUTER = "outer"
CORE = "core"


HEAD = 64
PAIR = 128


def pair_scores(info_ref, slope, q, k, score_scale):
    upper = info_ref[0]
    seq_length = info_ref[1]
    rows, cols = q.shape[0], k.shape[0]
    own = cols - rows
    raw = lax.dot_general(q, k, (((1,), (1,)), ((), ())), preferred_element_type=jnp.float32)
    query_pos = upper * rows + lax.broadcasted_iota(jnp.int32, (rows, cols), 0)
    key_index = lax.broadcasted_iota(jnp.int32, (rows, cols), 1)
    key_pos = jnp.where(key_index < own, key_index, upper * rows + key_index - own)
    allowed = ((key_index >= own) | (upper == 1)) & (key_pos < seq_length) & (key_pos <= query_pos)
    distance = (query_pos - key_pos).astype(jnp.float32)
    raw = raw * score_scale - slope * distance
    return jnp.where(allowed, raw, NEG_FILL)


def pair_fwd_kernel(score_scale, info_ref, slope_ref, q_ref, kr_ref, ko_ref, vr_ref, vo_ref, mix_ref, lse_ref):
    for head in range(PAIR // HEAD):
        cols = slice(head * HEAD, (head + 1) * HEAD)
        keys = jnp.concatenate([kr_ref[:, cols], ko_ref[:, cols]], 0)
        values = jnp.concatenate([vr_ref[:, cols], vo_ref[:, cols]], 0)
        slope = slope_ref[head][:, 0:1]
        scores = pair_scores(info_ref, slope, q_ref[:, cols], keys, score_scale)
        row_top = jnp.max(scores, axis=-1, keepdims=True)
        weights = jnp.exp(scores - row_top)
        row_total = jnp.sum(weights, axis=-1, keepdims=True)
        probs_low = (weights / row_total).astype(jnp.bfloat16)
        mix = jnp.dot(probs_low, values, preferred_element_type=jnp.float32)
        mix_ref[:, cols] = mix.astype(mix_ref.dtype)
        lse_ref[head] = row_top + jnp.log(row_total)


def pair_bwd_kernel(
    score_scale, info_ref, slope_ref, q_ref, kr_ref, ko_ref, vr_ref, vo_ref, g_ref, lse_ref,
    dq_ref, dkr_ref, dko_ref, dvr_ref, dvo_ref,
):
    rows = q_ref.shape[0]
    for head in range(PAIR // HEAD):
        cols = slice(head * HEAD, (head + 1) * HEAD)
        q = q_ref[:, cols]
        keys = jnp.concatenate([kr_ref[:, cols], ko_ref[:, cols]], 0)
        values = jnp.concatenate([vr_ref[:, cols], vo_ref[:, cols]], 0)
        grad = g_ref[:, cols]
        slope = slope_ref[head][:, 0:1]
        scores = pair_scores(info_ref, slope, q, keys, score_scale)
        probs = jnp.exp(scores - lse_ref[head])
        probs_low = probs.astype(jnp.bfloat16)
        dv = lax.dot_general(probs_low, grad, (((0,), (0,)), ((), ())), preferred_element_type=jnp.float32)
        grad_probs = lax.dot_general(grad, values, (((1,), (1,)), ((), ())), preferred_element_type=jnp.float32)
        row_delta = jnp.sum(probs * grad_probs, axis=-1, keepdims=True)
        grad_scores = (probs * (grad_probs - row_delta)).astype(jnp.bfloat16)
        dq_ref[:, cols] = jnp.dot(grad_scores, keys, preferred_element_type=jnp.float32) * score_scale
        dk = lax.dot_general(grad_scores, q, (((0,), (0,)), ((), ())), preferred_element_type=jnp.float32) * score_scale
        dkr_ref[:, cols] = dk[:rows]
        dko_ref[:, cols] = dk[rows:]
        dvr_ref[:, cols] = dv[:rows]
        dvo_ref[:, cols] = dv[rows:]


def slope_rows(slopes):
    return jnp.broadcast_to(slopes[:, None, None], (slopes.shape[0], 1, 128)).astype(jnp.float32)


def group_attention_fwd(info, slopes, queries, key_own, value_own, received, group, score_scale):
    rows = queries.shape[0]
    width = received.shape[1] // 2
    pairs = width // PAIR
    base = group * pairs
    full = lambda j, info_ref: (0, base + j)
    recv_k = lambda j, info_ref: (0, j)
    recv_v = lambda j, info_ref: (0, pairs + j)
    local = lambda j, info_ref: (0, j)
    per_pair = lambda j, info_ref: (j, 0, 0)
    heads = pairs * (PAIR // HEAD)
    return pl.pallas_call(
        functools.partial(pair_fwd_kernel, score_scale),
        grid_spec=pltpu.PrefetchScalarGridSpec(
            num_scalar_prefetch=1,
            grid=(pairs,),
            in_specs=[
                pl.BlockSpec((PAIR // HEAD, 1, 128), per_pair),
                pl.BlockSpec((rows, PAIR), full),
                pl.BlockSpec((rows, PAIR), recv_k),
                pl.BlockSpec((rows, PAIR), full),
                pl.BlockSpec((rows, PAIR), recv_v),
                pl.BlockSpec((rows, PAIR), full),
            ],
            out_specs=[
                pl.BlockSpec((rows, PAIR), local),
                pl.BlockSpec((PAIR // HEAD, rows, 1), per_pair),
            ],
        ),
        out_shape=[
            jax.ShapeDtypeStruct((rows, width), jnp.bfloat16),
            jax.ShapeDtypeStruct((heads, rows, 1), jnp.float32),
        ],
        compiler_params=pltpu.CompilerParams(vmem_limit_bytes=48 * 1024 * 1024),
        cost_estimate=pl.CostEstimate(
            flops=4 * heads * rows * 2 * rows * HEAD,
            transcendentals=heads * rows * 2 * rows,
            bytes_accessed=12 * rows * width,
        ),
    )(info, slope_rows(slopes), queries, received, key_own, received, value_own)


def group_attention_bwd(info, slopes, queries, key_own, value_own, received, grads, lse, group, score_scale):
    rows = queries.shape[0]
    width = received.shape[1] // 2
    pairs = width // PAIR
    base = group * pairs
    full = lambda j, info_ref: (0, base + j)
    recv_k = lambda j, info_ref: (0, j)
    recv_v = lambda j, info_ref: (0, pairs + j)
    local = lambda j, info_ref: (0, j)
    per_pair = lambda j, info_ref: (j, 0, 0)
    heads = pairs * (PAIR // HEAD)
    part = jax.ShapeDtypeStruct((rows, width), jnp.float32)
    return pl.pallas_call(
        functools.partial(pair_bwd_kernel, score_scale),
        grid_spec=pltpu.PrefetchScalarGridSpec(
            num_scalar_prefetch=1,
            grid=(pairs,),
            in_specs=[
                pl.BlockSpec((PAIR // HEAD, 1, 128), per_pair),
                pl.BlockSpec((rows, PAIR), full),
                pl.BlockSpec((rows, PAIR), recv_k),
                pl.BlockSpec((rows, PAIR), full),
                pl.BlockSpec((rows, PAIR), recv_v),
                pl.BlockSpec((rows, PAIR), full),
                pl.BlockSpec((rows, PAIR), full),
                pl.BlockSpec((PAIR // HEAD, rows, 1), per_pair),
            ],
            out_specs=[pl.BlockSpec((rows, PAIR), local)] * 5,
        ),
        out_shape=[part] * 5,
        compiler_params=pltpu.CompilerParams(vmem_limit_bytes=48 * 1024 * 1024),
        cost_estimate=pl.CostEstimate(
            flops=8 * heads * rows * 2 * rows * HEAD,
            transcendentals=heads * rows * 2 * rows,
            bytes_accessed=40 * rows * width,
        ),
    )(info, slope_rows(slopes), queries, received, key_own, received, value_own, grads, lse)


def passed_along(value, axis, steps):
    count = lax.axis_size(axis)
    leading, last = (max(0, -steps), min(count, count - steps))
    return lax.ppermute(value, axis, [(source, source + steps) for source in range(leading, last)])


SMALL_WIDTH = 3072


def small_rows(small_half, blocks):
    flat = small_half.reshape(-1)
    padded = blocks * SMALL_WIDTH
    return jnp.pad(flat, (0, padded - flat.shape[0])).reshape(blocks, 1, SMALL_WIDTH)


def gather_rows(row_arrays):
    cores = lax.axis_size(CORE)
    outer = lax.axis_size(OUTER)
    blocks = cores * outer
    place = lax.axis_index(CORE) * outer + lax.axis_index(OUTER)
    heights = [piece.shape[1] for piece in row_arrays]
    mine = jnp.concatenate(
        [lax.dynamic_index_in_dim(piece, place, 0, keepdims=False) for piece in row_arrays], 0
    )
    other = lax.ppermute(mine, SHARD, [(0, 1), (1, 0)])
    got = lax.all_gather(other, OUTER, axis=0, tiled=False)
    got = lax.all_gather(got, CORE, axis=0, tiled=False)
    got = got.reshape(blocks, -1, got.shape[-1])
    pieces = []
    offset = 0
    for height in heights:
        pieces.append(got[:, offset : offset + height])
        offset += height
    return pieces


def join_halves(own, other, dim):
    upper = lax.axis_index(SHARD) == 1
    in_order = jnp.concatenate([own, other], axis=dim)
    swapped = jnp.concatenate([other, own], axis=dim)
    return jnp.where(upper, swapped, in_order)


def reduce_rows(row_grads):
    shard_count = lax.axis_size(SHARD)
    cores = lax.axis_size(CORE)
    outer = lax.axis_size(OUTER)
    blocks = cores * outer
    heights = [piece.shape[3] for piece in row_grads]
    width = row_grads[0].shape[-1]
    stacked = jnp.concatenate([piece.astype(jnp.bfloat16) for piece in row_grads], 3)
    stacked = stacked.reshape(cores, -1, width)
    stacked = lax.psum_scatter(stacked, CORE, scatter_dimension=0, tiled=True)
    stacked = stacked.reshape(outer, -1, width)
    stacked = lax.psum_scatter(stacked, OUTER, scatter_dimension=0, tiled=True)
    stacked = stacked.reshape(shard_count, -1, width)
    stacked = lax.psum_scatter(stacked, SHARD, scatter_dimension=0, tiled=True)
    stacked = stacked.reshape(stacked.shape[1:])
    stacked = lax.all_gather(stacked, OUTER, axis=0, tiled=True)
    stacked = lax.all_gather(stacked, CORE, axis=0, tiled=True)
    stacked = stacked.reshape(blocks, -1, width)
    pieces = []
    offset = 0
    for height in heights:
        pieces.append(stacked[:, offset : offset + height].astype(jnp.float32))
        offset += height
    return pieces


def split_rows(grad_full):
    shard_count = lax.axis_size(SHARD)
    cores = lax.axis_size(CORE)
    outer = lax.axis_size(OUTER)
    rows, cols = grad_full.shape
    split = grad_full.reshape(shard_count, cores, outer, rows // (shard_count * cores * outer), cols)
    return split.transpose(1, 2, 0, 3, 4)


def block_major(grad_perm):
    shard_count = lax.axis_size(SHARD)
    cores = lax.axis_size(CORE)
    outer = lax.axis_size(OUTER)
    rows, cols = grad_perm.shape
    return grad_perm.reshape(cores, outer, shard_count, rows // (shard_count * cores * outer), cols)


def ff_order(values, blocks):
    shard_count = lax.axis_size(SHARD)
    rest = values.shape[1:]
    split = values.reshape((shard_count, blocks, values.shape[0] // (shard_count * blocks)) + rest)
    return jnp.swapaxes(split, 0, 1).reshape(values.shape)


def ff_natural(values, blocks):
    shard_count = lax.axis_size(SHARD)
    rest = values.shape[1:]
    split = values.reshape((blocks, shard_count, values.shape[0] // (shard_count * blocks)) + rest)
    return jnp.swapaxes(split, 0, 1).reshape(values.shape)


def join_blocks(own, other, blocks):
    upper = lax.axis_index(SHARD) == 1
    own_b = own.reshape((blocks, -1) + own.shape[1:])
    other_b = other.reshape((blocks, -1) + other.shape[1:])
    in_order = jnp.stack([own_b, other_b], 1)
    swapped = jnp.stack([other_b, own_b], 1)
    joined = jnp.where(upper, swapped, in_order)
    return joined.reshape((2 * own.shape[0],) + own.shape[1:])


def norm_stats(field_in):
    centred = field_in - jnp.mean(field_in, axis=-1, keepdims=True)
    inverse = lax.rsqrt(jnp.mean(centred * centred, axis=-1, keepdims=True) + EPS)
    return (centred * inverse, inverse)


def norm_back(grad_hat, normed, inverse):
    first_mean = jnp.mean(grad_hat, axis=-1, keepdims=True)
    second_mean = jnp.mean(grad_hat * normed, axis=-1, keepdims=True)
    return inverse * (grad_hat - first_mean - normed * second_mean)


def contract_rows(left_side, right_side):
    return lax.dot_general(
        left_side, right_side, (((0,), (0,)), ((), ())), preferred_element_type=jnp.float32
    )


def contract_cols(left_side, right_side):
    return lax.dot_general(
        left_side, right_side, (((1,), (1,)), ((), ())), preferred_element_type=jnp.float32
    )


def gelu_tanh(field_in):
    return jax.nn.gelu(field_in, approximate=True)


def gelu_back(pre_act, grad_act):
    _, pull_back = jax.vjp(gelu_tanh, pre_act)
    return pull_back(grad_act)[0]


def nesterov(grad_total, weight_old, moment_old, average_old, rate):
    moment_new = MOMENTUM * moment_old + grad_total
    weight_new = weight_old - rate * (grad_total + MOMENTUM * moment_new)
    average_new = AVERAGING * average_old + (1.0 - AVERAGING) * weight_new
    return (weight_new, moment_new, average_new)


def body(
    tokens,
    cotangent,
    lengths,
    qkv_weight,
    qkv_momentum,
    qkv_average,
    out_weight,
    out_momentum,
    out_average,
    up_weight,
    up_momentum,
    up_average,
    down_weight,
    down_momentum,
    down_average,
    small_params,
    small_momentum,
    small_average,
):
    tok_rows = tokens.shape[0]
    model_width = tokens.shape[1]
    shard_count = lax.axis_size(SHARD)
    group_count = lax.axis_size(OUTER) * lax.axis_size(CORE)
    shard_place = lax.axis_index(SHARD)
    group_place = lax.axis_index(OUTER) * lax.axis_size(CORE) + lax.axis_index(CORE)
    upper_half = shard_place % 2
    seq_place = group_place * (shard_count // 2) + shard_place // 2
    seq_length = lax.dynamic_index_in_dim(lengths, seq_place, 0, keepdims=False)
    local_pos = jnp.arange(tok_rows, dtype=jnp.int32)
    query_pos = upper_half * tok_rows + local_pos
    key_pos = jnp.concatenate([local_pos, query_pos])
    prev_live = jnp.full((tok_rows,), upper_half == 1)
    key_live = jnp.concatenate([prev_live, jnp.ones((tok_rows,), bool)]) & (key_pos < seq_length)
    distance = (query_pos[:, None] - key_pos[None, :]).astype(jnp.float32)
    row_live = (query_pos < seq_length).astype(jnp.float32)[:, None]
    head_size = model_width // HEADS
    score_scale = head_size ** (-0.5)
    slopes = 2.0 ** (-8.0 * (jnp.arange(HEADS, dtype=jnp.float32) + 1.0) / HEADS)
    blocks = lax.axis_size(CORE) * lax.axis_size(OUTER)
    qkv_own = qkv_weight.astype(jnp.bfloat16)
    small_own = small_params.astype(jnp.bfloat16)
    qkv_other, small_other = gather_rows(
        [qkv_own.reshape(blocks, -1, qkv_own.shape[1]), small_rows(small_own, blocks)]
    )
    qkv_full = join_halves(qkv_own, qkv_other.reshape(qkv_own.shape), 0)
    small_full = join_halves(
        small_own, small_other.reshape(-1)[: small_own.size].reshape(small_own.shape), 1
    )
    out_own = out_weight.astype(jnp.bfloat16)
    up_own_t = up_weight.astype(jnp.bfloat16).T
    down_own = down_weight.astype(jnp.bfloat16)
    out_other, up_other_t, down_other = gather_rows(
        [piece.reshape(blocks, -1, piece.shape[1]) for piece in (out_own, up_own_t, down_own)],
    )
    out_full = join_halves(out_own, out_other.reshape(out_own.shape), 0)
    up_full_t = join_blocks(up_own_t, up_other_t.reshape(up_own_t.shape), blocks)
    down_full = join_blocks(down_own, down_other.reshape(down_own.shape), blocks)
    table = small_full.astype(jnp.float32)
    up_bias = ff_order(table[8:12].reshape(FF), blocks)
    normed_one, inverse_one = norm_stats(tokens)
    entry_low = (normed_one * table[0] + table[1]).astype(jnp.bfloat16)
    mapped = jnp.dot(entry_low, qkv_full, preferred_element_type=jnp.float32)
    queries = (mapped[:, :model_width] + table[2]).astype(jnp.bfloat16)
    key_own = mapped[:, model_width : 2 * model_width].astype(jnp.bfloat16)
    value_own = (mapped[:, 2 * model_width :] + table[3]).astype(jnp.bfloat16)
    groups = 4
    per_group = HEADS // groups
    group_width = per_group * (model_width // HEADS)
    received_groups = []
    for group in range(groups):
        cols = slice(group * group_width, (group + 1) * group_width)
        received_groups.append(
            passed_along(jnp.concatenate([key_own[:, cols], value_own[:, cols]], 1), SHARD, 1)
        )

    info = jnp.stack([upper_half, seq_length]).astype(jnp.int32)
    fwd_parts = []
    for group in range(groups):
        chosen = slice(group * per_group, (group + 1) * per_group)
        fwd_parts.append(
            group_attention_fwd(
                info,
                slopes[chosen],
                queries,
                key_own,
                value_own,
                received_groups[group],
                group,
                score_scale,
            )
        )
    attended_low = jnp.concatenate([part[0] for part in fwd_parts], 1)
    resid_one = (
        tokens + jnp.dot(attended_low, out_full, preferred_element_type=jnp.float32) + table[4]
    )
    normed_two, inverse_two = norm_stats(resid_one)
    inner_low = (normed_two * table[5] + table[6]).astype(jnp.bfloat16)
    grad_out = cotangent * row_live
    down_bias_grad = jnp.sum(grad_out, axis=0)
    grad_low = grad_out.astype(jnp.bfloat16)
    pre_act = contract_cols(inner_low, up_full_t) + up_bias
    act_low = gelu_tanh(pre_act).astype(jnp.bfloat16)
    branch_out = jnp.dot(act_low, down_full, preferred_element_type=jnp.float32)
    block_out = resid_one + branch_out + table[7]
    grad_act = contract_cols(grad_low, down_full)
    down_grad = contract_rows(act_low, grad_low)
    grad_pre = gelu_back(pre_act, grad_act)
    up_bias_grad = ff_natural(jnp.sum(grad_pre, axis=0), blocks)
    pre_low = grad_pre.astype(jnp.bfloat16)
    up_grad_t = contract_rows(pre_low, inner_low)
    grad_inner = jnp.dot(pre_low, up_full_t, preferred_element_type=jnp.float32)
    gain_two_grad = jnp.sum(grad_inner * normed_two, axis=0)
    shift_two_grad = jnp.sum(grad_inner, axis=0)
    grad_resid = grad_out + norm_back(grad_inner * table[5], normed_two, inverse_two)
    resid_low = grad_resid.astype(jnp.bfloat16)
    out_grad = contract_rows(attended_low, resid_low)
    grad_resid, resid_low, up_grad_t, down_grad, out_grad = lax.optimization_barrier(
        (grad_resid, resid_low, up_grad_t, down_grad, out_grad)
    )
    out_sum, up_sum_t, down_sum = reduce_rows(
        [split_rows(out_grad), block_major(up_grad_t), block_major(down_grad)]
    )
    out_total = out_sum.reshape(out_weight.shape)
    up_total = up_sum_t.reshape(up_weight.shape[::-1]).T
    down_total = down_sum.reshape(down_weight.shape)
    out_bias_grad = jnp.sum(grad_resid, axis=0)
    grad_mixture = contract_cols(resid_low, out_full).astype(jnp.bfloat16)

    query_parts, key_parts, value_parts = [], [], []
    for group in range(groups):
        chosen = slice(group * per_group, (group + 1) * per_group)
        group_query, keys_back, keys_kept, values_back, values_kept = group_attention_bwd(
            info,
            slopes[chosen],
            queries,
            key_own,
            value_own,
            received_groups[group],
            grad_mixture,
            fwd_parts[group][1],
            group,
            score_scale,
        )
        returned = passed_along(
            jnp.concatenate([keys_back, values_back], 1).astype(jnp.bfloat16), SHARD, -1
        ).astype(jnp.float32)
        query_parts.append(group_query)
        key_parts.append(keys_kept + returned[:, :group_width])
        value_parts.append(values_kept + returned[:, group_width:])
    grad_query = jnp.concatenate(query_parts, 1)
    grad_key_own = jnp.concatenate(key_parts, 1)
    grad_value_own = jnp.concatenate(value_parts, 1)
    query_bias_grad = jnp.sum(grad_query, axis=0)
    value_bias_grad = jnp.sum(grad_value_own, axis=0)
    mapped_low = jnp.concatenate([grad_query, grad_key_own, grad_value_own], 1).astype(jnp.bfloat16)
    qkv_grad = contract_rows(entry_low, mapped_low)
    grad_entry = contract_cols(mapped_low, qkv_full)
    gain_one_grad = jnp.sum(grad_entry * normed_one, axis=0)
    shift_one_grad = jnp.sum(grad_entry, axis=0)
    input_grad = grad_resid + norm_back(grad_entry * table[0], normed_one, inverse_one)
    head_rows = jnp.stack(
        [
            gain_one_grad,
            shift_one_grad,
            query_bias_grad,
            value_bias_grad,
            out_bias_grad,
            gain_two_grad,
            shift_two_grad,
            down_bias_grad,
        ]
    )
    small_grad = jnp.concatenate([head_rows, up_bias_grad.reshape(4, model_width)], 0)
    small_halves = small_grad.reshape(small_grad.shape[0], shard_count, -1).transpose(1, 0, 2)
    small_packed = jnp.stack(
        [small_rows(small_halves[index], blocks) for index in range(shard_count)]
    ).reshape(shard_count, lax.axis_size(CORE), lax.axis_size(OUTER), 1, SMALL_WIDTH)
    small_packed = small_packed.transpose(1, 2, 0, 3, 4)
    qkv_sum, small_sum = reduce_rows([split_rows(qkv_grad), small_packed])
    qkv_total = qkv_sum.reshape(qkv_weight.shape)
    small_total = small_sum.reshape(-1)[: small_params.size].reshape(small_params.shape)
    rate = 2.0 / math.sqrt(model_width * tok_rows * shard_count * group_count)
    qkv_new = nesterov(qkv_total, qkv_weight, qkv_momentum, qkv_average, rate)
    out_new = nesterov(out_total, out_weight, out_momentum, out_average, rate)
    up_new = nesterov(up_total, up_weight, up_momentum, up_average, rate)
    down_new = nesterov(down_total, down_weight, down_momentum, down_average, rate)
    small_new = nesterov(small_total, small_params, small_momentum, small_average, rate)
    return (
        block_out,
        input_grad,
        qkv_new[0],
        qkv_new[1],
        qkv_new[2],
        out_new[0],
        out_new[1],
        out_new[2],
        up_new[0],
        up_new[1],
        up_new[2],
        down_new[0],
        down_new[1],
        down_new[2],
        small_new[0],
        small_new[1],
        small_new[2],
    )


def solution(mesh):
    cores = 2
    devices = mesh.devices.reshape(mesh.shape["group"] // cores, cores, mesh.shape[SHARD])
    inner_mesh = jax.sharding.Mesh(devices, (OUTER, CORE, SHARD))
    rows = P((OUTER, CORE, SHARD), None)
    in_specs = (
        rows,
        rows,
        P(),
        P(SHARD, None),
        P(SHARD, None),
        P(SHARD, None),
        P(SHARD, None),
        P(SHARD, None),
        P(SHARD, None),
        P(None, SHARD),
        P(None, SHARD),
        P(None, SHARD),
        P(SHARD, None),
        P(SHARD, None),
        P(SHARD, None),
        P(None, SHARD),
        P(None, SHARD),
        P(None, SHARD),
    )
    out_specs = (
        rows,
        rows,
        P(SHARD, None),
        P(SHARD, None),
        P(SHARD, None),
        P(SHARD, None),
        P(SHARD, None),
        P(SHARD, None),
        P(None, SHARD),
        P(None, SHARD),
        P(None, SHARD),
        P(SHARD, None),
        P(SHARD, None),
        P(SHARD, None),
        P(None, SHARD),
        P(None, SHARD),
        P(None, SHARD),
    )

    return jax.shard_map(body, mesh=inner_mesh, in_specs=in_specs, out_specs=out_specs, check_vma=False)
```

profile of v0, /device:TPU:9, one launch (start us, length us, event | category | flops | bytes accessed | tf_op | source)
XLA Modules:
  0.0 1063.4 jit_solution(11872924715013578333)
XLA Ops:
  40.7 12.3 %collective-permute-done.5 = bf16[288,1024]{1,0:T(8,128)(2,1)S(1)} collective-permute-done((bf16[288,1024]{1,0:T(8,128)(2,1)S(1)}, bf16[288,1024]{1,0:T(8,128)(2,1)S(1)}, u32[]{:S(2)}, u32[]{:S(2)}) %collective-permute-start.5) | collective-permute-done | bytes 589856 | tf_op jit(solution)/shard_map/ppermute | solution.py:196
  53.9 16.9 %all-gather.32.cloned.1.call-done = bf16[8,33,3072]{2,1,0:T(8,128)(2,1)} async-done(((bf16[1,33,3072]{2,1,0:T(8,128)(2,1)}), bf16[8,33,3072]{2,1,0:T(8,128)(2,1)}) %all-gather.32.cloned.1.call-update) | async-done | bytes 1622032 | tf_op jit(solution)/shard_map/all_gather | solution.py:197
  74.5 75.6 %all-gather.20.cloned.1.call-done = bf16[2304,1024]{1,0:T(8,128)(2,1)} async-done(((bf16[288,1024]{1,0:T(8,128)(2,1)}), bf16[2304,1024]{1,0:T(8,128)(2,1)}) %all-gather.20.cloned.1.call-update) | async-done | bytes 4718608 | tf_op jit(solution)/shard_map/all_gather | solution.py:197
  151.4 14.6 %all-gather.18.cloned.1.call-done = bf16[16,33,3072]{2,0,1:T(8,128)(2,1)} async-done(((bf16[8,33,3072]{2,0,1:T(8,128)(2,1)}), bf16[16,33,3072]{2,0,1:T(8,128)(2,1)}) %all-gather.18.cloned.1.call-update) | async-done | bytes 3244048 | tf_op jit(solution)/shard_map/all_gather | solution.py:198
  198.2 21.2 %collective-permute-done.4.kr_ref.vr_ref = bf16[512,512]{1,0:T(8,128)(2,1)} collective-permute-done((bf16[512,512]{1,0:T(8,128)(2,1)}, bf16[512,512]{1,0:T(8,128)(2,1)}, u32[]{:S(2)}, u32[]{:S(2)}) %collective-permute-start.4) | collective-permute-done | bytes 524320 | tf_op jit(solution)/shard_map/ppermute | solution.py:175
  272.9 13.6 %fusion.39 = f32[512,4096]{1,0:T(8,128)} fusion(bf16[4096,1024]{1,0:T(8,128)(2,1)} %bitcast.124, f32[512,1024]{1,0:T(8,128)S(1)} %get-tuple-element.150, f32[1024]{0:T(1024)S(1)} %bitcast.158, f32[1024]{0:T(1024)S(1)} %bitcast.145, f32[512]{0:T(512)S(1)} %add_rsqrt_fusion, f32[512]{0:T(512)S(1)} %broadcast_multiply_fusion.4), kind=kOutput, calls=%fused_computation.154 | convolution fusion | flops 4297588736 | bytes 18886656 | tf_op jit(solution)/shard_map/dot_general | solution.py:301
  286.5 14.0 %fusion.37 = bf16[4096,1024]{1,0:T(8,128)(2,1)} fusion(f32[512,1024]{1,0:T(8,128)} %param.19, f32[512]{0:T(512)S(1)} %fusion.32, f32[512,4096]{1,0:T(8,128)} %fusion.39, f32[4096]{0:T(1024)S(1)} %bitcast.151), kind=kOutput, calls=%fused_computation.152 | convolution fusion | flops 4316987392 | bytes 18892800 | tf_op jit(solution)/shard_map/dot_general | solution.py:295
  300.5 12.3 %fusion.53 = (bf16[4096]{0:T(1024)(128)(2,1)S(1)}, bf16[512,4096]{1,0:T(8,128)(2,1)S(1)}) fusion(f32[512,4096]{1,0:T(8,128)} %fusion.39, f32[4096]{0:T(1024)S(1)} %bitcast.152, bf16[4096,1024]{1,0:T(8,128)(2,1)S(1)} %bitcast.122, f32[512,1024]{1,0:T(8,128)} %param.19, f32[512]{0:T(512)S(1)} %fusion.32), kind=kOutput, calls=%fused_computation.164 | convolution fusion | flops 4342149120 | bytes 23095296 | tf_op jit(solution)/shard_map/dot_general | solution.py:301
  341.2 11.2 %shard_map.312 = (f32[512,256]{1,0:T(8,128)S(1)}, f32[512,256]{1,0:T(8,128)S(1)}, f32[512,256]{1,0:T(8,128)S(1)}, f32[512,256]{1,0:T(8,128)S(1)}, f32[512,256]{1,0:T(8,128)S(1)}) custom-call(s32[2]{0:T(128)S(1)} %pad_add_fusion.info_ref, f32[4,1,128]{2,1,0:T(1,128)S(1)} %broadcast_in_dim.19.slope_ref, bf16[512,1024]{1,0:T(8,128)(2,1)S(1)} %get-tuple-element.123.q_ref, ...), custom_call_target="tpu_custom_call" | custom-call | flops 1073741824 | bytes 5242880 | tf_op jit(solution)/shard_map/pallas_call | solution.py:145
  354.8 11.4 %shard_map.311 = (f32[512,256]{1,0:T(8,128)S(1)}, f32[512,256]{1,0:T(8,128)S(1)}, f32[512,256]{1,0:T(8,128)S(1)}, f32[512,256]{1,0:T(8,128)S(1)}, f32[512,256]{1,0:T(8,128)S(1)}) custom-call(s32[2]{0:T(128)S(1)} %pad_add_fusion.info_ref, f32[4,1,128]{2,1,0:T(1,128)S(1)} %broadcast_in_dim.18.slope_ref, bf16[512,1024]{1,0:T(8,128)(2,1)S(1)} %get-tuple-element.123.q_ref, ...), custom_call_target="tpu_custom_call" | custom-call | flops 1073741824 | bytes 5242880 | tf_op jit(solution)/shard_map/pallas_call | solution.py:145
  368.7 11.2 %shard_map.310 = (f32[512,256]{1,0:T(8,128)S(1)}, f32[512,256]{1,0:T(8,128)S(1)}, f32[512,256]{1,0:T(8,128)S(1)}, f32[512,256]{1,0:T(8,128)S(1)}, f32[512,256]{1,0:T(8,128)S(1)}) custom-call(s32[2]{0:T(128)S(1)} %pad_add_fusion.info_ref, f32[4,1,128]{2,1,0:T(1,128)S(1)} %broadcast_in_dim.17.slope_ref, bf16[512,1024]{1,0:T(8,128)(2,1)S(1)} %get-tuple-element.123.q_ref, ...), custom_call_target="tpu_custom_call" | custom-call | flops 1073741824 | bytes 5242880 | tf_op jit(solution)/shard_map/pallas_call | solution.py:145
  443.9 11.9 %copy.100 = bf16[2,2,8,32,3072]{4,1,3,0,2:T(2,128)(2,1)S(1)} copy(bf16[2,2,8,32,3072]{4,3,2,1,0:T(8,128)(2,1)} %bitcast.129) | data formatting | bytes 12582912 | tf_op jit(solution)/shard_map/convert_element_type | solution.py:222
  471.1 15.1 %pad_maximum_fusion = bf16[2,8,2,288,1024]{4,3,2,1,0:T(8,128)(2,1)} fusion(bf16[2,8,2,128,1024]{4,3,2,1,0:T(8,128)(2,1)} %bitcast.127, bf16[2,8,2,128,1024]{4,3,2,1,0:T(8,128)(2,1)} %bitcast.128, bf16[2,8,2,32,1024]{4,3,2,1,0:T(8,128)(2,1)S(1)} %bitcast.126), kind=kLoop, calls=%fused_computation | loop fusion | flops 56623104 | bytes 37748736 | tf_op jit(solution)/shard_map/concatenate | solution.py:222
  490.0 26.7 %reduce-scatter.13.cloned.1.call-done = bf16[1,4608,1024]{2,1,0:T(8,128)(2,1)} async-done(((bf16[2,4608,1024]{2,1,0:T(8,128)(2,1)}), bf16[1,4608,1024]{2,1,0:T(8,128)(2,1)}) %reduce-scatter.13.cloned.1.call-update) | async-done | bytes 9437200 | tf_op jit(solution)/shard_map/reduce_scatter | solution.py:224
  516.8 83.6 %reduce-scatter.9.cloned.1.call-done = bf16[1,66,3072]{2,1,0:T(8,128)(2,1)} async-done(((bf16[8,66,3072]{2,1,0:T(8,128)(2,1)}), bf16[1,66,3072]{2,1,0:T(8,128)(2,1)}) %reduce-scatter.9.cloned.1.call-update) | async-done | bytes 405520 | tf_op jit(solution)/shard_map/reduce_scatter | solution.py:226
  602.4 162.5 %reduce-scatter.15.cloned.1.call-done = bf16[1,576,1024]{2,1,0:T(8,128)(2,1)} async-done(((bf16[8,576,1024]{2,1,0:T(8,128)(2,1)}), bf16[1,576,1024]{2,1,0:T(8,128)(2,1)}) %reduce-scatter.15.cloned.1.call-update) | async-done | bytes 1179664 | tf_op jit(solution)/shard_map/reduce_scatter | solution.py:226
  765.0 17.5 %reduce-scatter.11.cloned.1.call-done = bf16[1,33,3072]{2,1,0:T(8,128)(2,1)} async-done(((bf16[2,33,3072]{2,1,0:T(8,128)(2,1)}), bf16[1,33,3072]{2,1,0:T(8,128)(2,1)}) %reduce-scatter.11.cloned.1.call-update) | async-done | bytes 202768 | tf_op jit(solution)/shard_map/reduce_scatter | solution.py:228
  784.5 21.9 %reduce-scatter.17.cloned.1.call-done = bf16[1,288,1024]{2,1,0:T(8,128)(2,1)} async-done(((bf16[2,288,1024]{2,1,0:T(8,128)(2,1)}), bf16[1,288,1024]{2,1,0:T(8,128)(2,1)}) %reduce-scatter.17.cloned.1.call-update) | async-done | bytes 589840 | tf_op jit(solution)/shard_map/reduce_scatter | solution.py:228
  806.5 62.4 %all-gather.24.cloned.1.call-done = bf16[1,264,3072]{2,0,1:T(2,128)(2,1)} async-done(((bf16[1,33,3072]{2,0,1:T(2,128)(2,1)}), bf16[1,264,3072]{2,0,1:T(2,128)(2,1)}) %all-gather.24.cloned.1.call-update) | async-done | bytes 1622032 | tf_op jit(solution)/shard_map/all_gather | solution.py:230
  872.6 75.5 %all-gather.28.cloned.1.call-done = bf16[1,2304,1024]{2,1,0:T(8,128)(2,1)} async-done(((bf16[1,288,1024]{2,1,0:T(8,128)(2,1)}), bf16[1,2304,1024]{2,1,0:T(8,128)(2,1)}) %all-gather.28.cloned.1.call-update) | async-done | bytes 4718608 | tf_op jit(solution)/shard_map/all_gather | solution.py:230
  948.2 12.6 %add_add_fusion = f32[512,1024]{1,0:T(8,128)} fusion(f32[512,1024]{1,0:T(8,128)S(1)} %copy-done.29, bf16[4096,1024]{1,0:T(8,128)(2,1)} %bitcast.123, f32[1024]{0:T(1024)S(1)} %bitcast.155, f32[512,4096]{1,0:T(8,128)} %fusion.39, f32[4096]{0:T(1024)S(1)} %bitcast.153), kind=kOutput, calls=%fused_computation.58 | convolution fusion | flops 4316987392 | bytes 20992000 | tf_op jit(solution)/shard_map/dot_general | solution.py:425
  971.9 17.4 %multiply_add_fusion.2 = (f32[512,3072]{1,0:T(8,128)}, f32[512,3072]{1,0:T(8,128)}, f32[512,3072]{1,0:T(8,128)}) fusion(f32[512,3072]{1,0:T(8,128)} %param.23, f32[512,3072]{1,0:T(8,128)} %param.21, bf16[16,32,3072]{2,1,0:T(8,128)(2,1)S(1)} %slice.239, f32[512,3072]{1,0:T(8,128)} %param.22), kind=kLoop, calls=%fused_computation.29 | loop fusion | flops 15728640 | bytes 40894464 | tf_op jit(solution)/shard_map/add | solution.py:318
  1015.7 22.3 %multiply_add_fusion.1 = (f32[1024,2048]{1,0:T(8,128)}, f32[1024,2048]{1,0:T(8,128)}, f32[1024,2048]{1,0:T(8,128)}) fusion(f32[1024,2048]{1,0:T(8,128)} %param.29, f32[1024,2048]{1,0:T(8,128)} %param.27, f32[2048,1024]{0,1:T(8,128)} %copy.96, f32[1024,2048]{1,0:T(8,128)} %param.28), kind=kLoop, calls=%fused_computation.20 | loop fusion | flops 18874368 | bytes 58720256 | tf_op jit(solution)/shard_map/add | solution.py:318
  1038.0 18.6 %multiply_add_fusion = (f32[2048,1024]{1,0:T(8,128)}, f32[2048,1024]{1,0:T(8,128)}, f32[2048,1024]{1,0:T(8,128)}) fusion(f32[2048,1024]{1,0:T(8,128)} %param.32, f32[2048,1024]{1,0:T(8,128)} %param.30, bf16[16,128,1024]{2,1,0:T(8,128)(2,1)} %get-tuple-element.118, f32[2048,1024]{1,0:T(8,128)} %param.31), kind=kLoop, calls=%fused_computation.19 | loop fusion | flops 20971520 | bytes 54525952 | tf_op jit(solution)/shard_map/add | solution.py:318
  (307 shorter events, 285.7 us)
Async XLA Ops:
  7.2 63.7 %all-gather.32.cloned.1.call-start = ((), (), s32[]{:S(2)}) async-start(), calls=%async_computation.19 | async-start | bytes 2211840 | tf_op jit(solution)/shard_map/all_gather | solution.py:197
  14.2 6.9 collective-permute-start
  21.8 128.3 %all-gather.20.cloned.1.call-start = ((), (), s32[]{:S(2)}) async-start(), calls=%async_computation.13 | async-start | bytes 5308416 | tf_op jit(solution)/shard_map/all_gather | solution.py:197
  39.4 13.6 %collective-permute-start.5 = (bf16[288,1024]{1,0:T(8,128)(2,1)S(1)}, bf16[288,1024]{1,0:T(8,128)(2,1)S(1)}, u32[]{:S(2)}, u32[]{:S(2)}) collective-permute-start(bf16[288,1024]{1,0:T(8,128)(2,1)S(1)} %pad_maximum_fusion.2), channel_id=1, source_target_pairs={{0,1},{1,0},{2,3},{3,2},{4,5},{5,4},{6,7},{7,6},{8,9},{9,8},{10,11... | collective-permute-start | bytes 1769480 | tf_op jit(solution)/shard_map/ppermute | solution.py:196
  53.9 112.1 %all-gather.18.cloned.1.call-start = ((), (), s32[]{:S(2)}) async-start(), calls=%async_computation.12 | async-start | bytes 4866048 | tf_op jit(solution)/shard_map/all_gather | solution.py:198
  74.5 184.4 %all-gather.22.cloned.1.call-start = ((), (), s32[]{:S(2)}) async-start(), calls=%async_computation.14 | async-start | bytes 14155776 | tf_op jit(solution)/shard_map/all_gather | solution.py:198
  150.1 336.2 %reduce-scatter.7.cloned.1.call-start = ((), (), s32[]{:S(2)}) async-start(), calls=%async_computation.6 | async-start | bytes 9732096 | tf_op jit(solution)/shard_map/reduce_scatter | solution.py:224
  182.3 64.4 %collective-permute-start.1 = (bf16[512,512]{1,0:T(8,128)(2,1)}, bf16[512,512]{1,0:T(8,128)(2,1)}, u32[]{:S(2)}, u32[]{:S(2)}) collective-permute-start(bf16[512,512]{1,0:T(8,128)(2,1)} %pad_maximum_fusion.3), channel_id=1, source_target_pairs={{0,1},{2,3},{4,5},{6,7},{8,9},{10,11},{12,13},{14,15},{16,17},{18,... | collective-permute-start | bytes 1572872 | tf_op jit(solution)/shard_map/ppermute | solution.py:175
  187.1 41.4 %collective-permute-start.3 = (bf16[512,512]{1,0:T(8,128)(2,1)}, bf16[512,512]{1,0:T(8,128)(2,1)}, u32[]{:S(2)}, u32[]{:S(2)}) collective-permute-start(bf16[512,512]{1,0:T(8,128)(2,1)} %pad_maximum_fusion.5), channel_id=1, source_target_pairs={{0,1},{2,3},{4,5},{6,7},{8,9},{10,11},{12,13},{14,15},{16,17},{18,... | collective-permute-start | bytes 1572872 | tf_op jit(solution)/shard_map/ppermute | solution.py:175
  190.0 29.4 %collective-permute-start.4 = (bf16[512,512]{1,0:T(8,128)(2,1)}, bf16[512,512]{1,0:T(8,128)(2,1)}, u32[]{:S(2)}, u32[]{:S(2)}) collective-permute-start(bf16[512,512]{1,0:T(8,128)(2,1)} %pad_maximum_fusion.6), channel_id=1, source_target_pairs={{0,1},{2,3},{4,5},{6,7},{8,9},{10,11},{12,13},{14,15},{16,17},{18,... | collective-permute-start | bytes 1572872 | tf_op jit(solution)/shard_map/ppermute | solution.py:175
  192.9 44.7 %collective-permute-start.2 = (bf16[512,512]{1,0:T(8,128)(2,1)}, bf16[512,512]{1,0:T(8,128)(2,1)}, u32[]{:S(2)}, u32[]{:S(2)}) collective-permute-start(bf16[512,512]{1,0:T(8,128)(2,1)} %pad_maximum_fusion.4), channel_id=1, source_target_pairs={{0,1},{2,3},{4,5},{6,7},{8,9},{10,11},{12,13},{14,15},{16,17},{18,... | collective-permute-start | bytes 1572872 | tf_op jit(solution)/shard_map/ppermute | solution.py:175
  353.5 68.0 %collective-permute-start.9 = (bf16[512,512]{1,0:T(8,128)(2,1)}, bf16[512,512]{1,0:T(8,128)(2,1)S(1)}, u32[]{:S(2)}, u32[]{:S(2)}) collective-permute-start(bf16[512,512]{1,0:T(8,128)(2,1)} %pad_maximum_fusion.10), channel_id=1, source_target_pairs={{1,0},{3,2},{5,4},{7,6},{9,8},{11,10},{13,12},{15,14},{17,16},{19,... | collective-permute-start | bytes 1572872 | tf_op jit(solution)/shard_map/ppermute | solution.py:175
  367.4 43.3 %collective-permute-start.8 = (bf16[512,512]{1,0:T(8,128)(2,1)}, bf16[512,512]{1,0:T(8,128)(2,1)}, u32[]{:S(2)}, u32[]{:S(2)}) collective-permute-start(bf16[512,512]{1,0:T(8,128)(2,1)} %pad_maximum_fusion.9), channel_id=1, source_target_pairs={{1,0},{3,2},{5,4},{7,6},{9,8},{11,10},{13,12},{15,14},{17,16},{19,... | collective-permute-start | bytes 1572872 | tf_op jit(solution)/shard_map/ppermute | solution.py:175
  393.6 15.1 %collective-permute-start.6 = (bf16[512,512]{1,0:T(8,128)(2,1)}, bf16[512,512]{1,0:T(8,128)(2,1)S(1)}, u32[]{:S(2)}, u32[]{:S(2)}) collective-permute-start(bf16[512,512]{1,0:T(8,128)(2,1)} %pad_maximum_fusion.7), channel_id=1, source_target_pairs={{1,0},{3,2},{5,4},{7,6},{9,8},{11,10},{13,12},{15,14},{17,16},{19,... | collective-permute-start | bytes 1572872 | tf_op jit(solution)/shard_map/ppermute | solution.py:175
  395.7 24.2 %collective-permute-start.7 = (bf16[512,512]{1,0:T(8,128)(2,1)}, bf16[512,512]{1,0:T(8,128)(2,1)S(1)}, u32[]{:S(2)}, u32[]{:S(2)}) collective-permute-start(bf16[512,512]{1,0:T(8,128)(2,1)} %pad_maximum_fusion.8), channel_id=1, source_target_pairs={{1,0},{3,2},{5,4},{7,6},{9,8},{11,10},{13,12},{15,14},{17,16},{19,... | collective-permute-start | bytes 1572872 | tf_op jit(solution)/shard_map/ppermute | solution.py:175
  469.3 47.5 %reduce-scatter.13.cloned.1.call-start = ((), (), s32[]{:S(2)}) async-start(), calls=%async_computation.9 | async-start | bytes 28311552 | tf_op jit(solution)/shard_map/reduce_scatter | solution.py:224
  486.2 114.2 %reduce-scatter.9.cloned.1.call-start = ((), (), s32[]{:S(2)}) async-start(), calls=%async_computation.7 | async-start | bytes 3981312 | tf_op jit(solution)/shard_map/reduce_scatter | solution.py:226
  490.0 274.9 %reduce-scatter.15.cloned.1.call-start = ((), (), s32[]{:S(2)}) async-start(), calls=%async_computation.10 | async-start | bytes 10616832 | tf_op jit(solution)/shard_map/reduce_scatter | solution.py:226
  516.8 265.7 %reduce-scatter.11.cloned.1.call-start = ((), (), s32[]{:S(2)}) async-start(), calls=%async_computation.8 | async-start | bytes 737280 | tf_op jit(solution)/shard_map/reduce_scatter | solution.py:228
  602.3 204.1 %reduce-scatter.17.cloned.1.call-start = ((), (), s32[]{:S(2)}) async-start(), calls=%async_computation.11 | async-start | bytes 1769472 | tf_op jit(solution)/shard_map/reduce_scatter | solution.py:228
  764.9 104.0 %all-gather.24.cloned.1.call-start = ((), (), s32[]{:S(2)}) async-start(), calls=%async_computation.15 | async-start | bytes 3649536 | tf_op jit(solution)/shard_map/all_gather | solution.py:230
  784.5 163.7 %all-gather.28.cloned.1.call-start = ((), (), s32[]{:S(2)}) async-start(), calls=%async_computation.17 | async-start | bytes 5308416 | tf_op jit(solution)/shard_map/all_gather | solution.py:230
  806.4 157.6 %all-gather.26.cloned.1.call-start = ((), (), s32[]{:S(2)}) async-start(), calls=%async_computation.16 | async-start | bytes 4866048 | tf_op jit(solution)/shard_map/all_gather | solution.py:231
  872.5 116.8 %all-gather.30.cloned.1.call-start = ((), (), s32[]{:S(2)}) async-start(), calls=%async_computation.18 | async-start | bytes 14155776 | tf_op jit(solution)/shard_map/all_gather | solution.py:231
  (53 other events, 757.7 us)
Sparse Core Ops, SparseCore 0:
  21.9 48.8 all-gather.31
  73.6 76.4 all-gather.19
  152.2 13.7 all-gather.17
  167.4 22.7 all-gather.21
  469.4 16.4 reduce-scatter.6
  488.1 28.6 reduce-scatter.12
  521.0 79.4 reduce-scatter.8
  604.0 160.8 reduce-scatter.14
  767.8 14.6 reduce-scatter.10
  784.5 21.8 reduce-scatter.16
  809.2 59.7 all-gather.23
  871.0 77.1 all-gather.27
  950.3 13.7 all-gather.25
  965.4 22.7 all-gather.29
where the time goes:
time: 1070 us; the launch traced here: 1060 us
  waiting for transfers between devices  616 us (58%)
  other arithmetic  146 us (14%)
  matrix products  101 us (9%)
  local copies, waits for them, and re-layouts  88.1 us (8%)
  Pallas kernels  77.5 us (7%)
  starting transfers between devices  19.4 us (2%)
  between operations  15.2 us (1%)
    reduce_scatter x2, waiting for transfers between devices, reduce_rows(): stacked = lax.psum_scatter(stacked, OUTER, scatter_dimension=0, tiled=True)  246 us
    all_gather x2, waiting for transfers between devices, reduce_rows(): stacked = lax.all_gather(stacked, OUTER, axis=0, tiled=True)  138 us
    all_gather x2, waiting for transfers between devices, gather_rows(): got = lax.all_gather(other, OUTER, axis=0, tiled=False)  92.5 us
    add x5, other arithmetic, nesterov(): average_new = AVERAGING * average_old + (1.0 - AVERAGING) * weight_new  64.8 us
    pallas_call x4, Pallas kernels, group_attention_bwd(): pl.pallas_call(functools.partial(pair_bwd_kernel, score_scale), grid_spec...  45.1 us
    reduce_scatter x2, waiting for transfers between devices, reduce_rows(): stacked = lax.psum_scatter(stacked, SHARD, scatter_dimension=0, tiled=True)  39.3 us
    ppermute x8, waiting for transfers between devices, passed_along(): lax.ppermute(value, axis, [(source, source + steps) for source in range(l...  37.5 us
    dot_general x4, matrix products, contract_cols(): lax.dot_general(left_side, right_side, (((1,), (1,)), ((), ())), preferre...  35.4 us
  transfers between devices with their start and end apart: 24, of which 16 were waited for; matrix products, arithmetic and copies ran while one was open for 11% of the time, Pallas kernels for 6%

commit v1 on v0

--- a/solution.py
+++ b/solution.py
@@ -184,6 +184,21 @@
     return jnp.pad(flat, (0, padded - flat.shape[0])).reshape(blocks, 1, SMALL_WIDTH)
 
 
+def gather_ring(piece, axis):
+    count = lax.axis_size(axis)
+    place = lax.axis_index(axis)
+    held = piece[None]
+    step = 1
+    while step < count:
+        received = lax.ppermute(held, axis, [(index, index ^ step) for index in range(count)])
+        first = (place & step) == 0
+        held = jnp.where(
+            first, jnp.concatenate([held, received], 0), jnp.concatenate([received, held], 0)
+        )
+        step *= 2
+    return held
+
+
 def gather_rows(row_arrays):
     cores = lax.axis_size(CORE)
     outer = lax.axis_size(OUTER)
@@ -195,7 +210,7 @@
     )
     other = lax.ppermute(mine, SHARD, [(0, 1), (1, 0)])
     got = lax.all_gather(other, OUTER, axis=0, tiled=False)
-    got = lax.all_gather(got, CORE, axis=0, tiled=False)
+    got = gather_ring(got, CORE)
     got = got.reshape(blocks, -1, got.shape[-1])
     pieces = []
     offset = 0
@@ -212,7 +227,7 @@
     return jnp.where(upper, swapped, in_order)
 
 
-def reduce_rows(row_grads):
+def reduce_rows(row_grads, core_on_dma=False):
     shard_count = lax.axis_size(SHARD)
     cores = lax.axis_size(CORE)
     outer = lax.axis_size(OUTER)
@@ -228,7 +243,10 @@
     stacked = lax.psum_scatter(stacked, SHARD, scatter_dimension=0, tiled=True)
     stacked = stacked.reshape(stacked.shape[1:])
     stacked = lax.all_gather(stacked, OUTER, axis=0, tiled=True)
-    stacked = lax.all_gather(stacked, CORE, axis=0, tiled=True)
+    if core_on_dma:
+        stacked = gather_ring(stacked, CORE)
+    else:
+        stacked = lax.all_gather(stacked, CORE, axis=0, tiled=True)
     stacked = stacked.reshape(blocks, -1, width)
     pieces = []
     offset = 0
@@ -440,7 +458,7 @@
         (grad_resid, resid_low, up_grad_t, down_grad, out_grad)
     )
     out_sum, up_sum_t, down_sum = reduce_rows(
-        [split_rows(out_grad), block_major(up_grad_t), block_major(down_grad)]
+        [split_rows(out_grad), block_major(up_grad_t), block_major(down_grad)], core_on_dma=True
     )
     out_total = out_sum.reshape(out_weight.shape)
     up_total = up_sum_t.reshape(up_weight.shape[::-1]).T
@@ -498,7 +516,7 @@
         [small_rows(small_halves[index], blocks) for index in range(shard_count)]
     ).reshape(shard_count, lax.axis_size(CORE), lax.axis_size(OUTER), 1, SMALL_WIDTH)
     small_packed = small_packed.transpose(1, 2, 0, 3, 4)
-    qkv_sum, small_sum = reduce_rows([split_rows(qkv_grad), small_packed])
+    qkv_sum, small_sum = reduce_rows([split_rows(qkv_grad), small_packed], core_on_dma=True)
     qkv_total = qkv_sum.reshape(qkv_weight.shape)
     small_total = small_sum.reshape(-1)[: small_params.size].reshape(small_params.shape)
     rate = 2.0 / math.sqrt(model_width * tok_rows * shard_count * group_count)

time: 1070 us -> 1080 us (level)
  other arithmetic: 146 us -> 175 us
  waiting for transfers between devices: 616 us -> 591 us
    select_n x0 -> x4, other arithmetic: none -> 33.4 us  [gather_ring(): jnp.where(first, jnp.concatenate([held, received], 0), jnp.concatenate([r...]
    all_gather x4 -> x0, waiting for transfers between devices: 17.9 us -> none  [the longest x2 14.6 us: gather_rows(): got = lax.all_gather(got, CORE, axis=0, tiled=False)]
    select_n x0 -> x3, local copies, waits for them, and re-layouts: none -> 11.8 us  [the longest x1 8.52 us: join_blocks(): joined = jnp.where(upper, swapped, in_order)]
  transfers between devices with their start and end apart: 24 -> 24, of which waited for: 16 -> 14; matrix products, arithmetic and copies ran while one was open for 11% -> 12% of each run, Pallas kernels for 6% -> 6%
where the time goes in v1:
time: 1080 us; the launch traced here: 1070 us
  waiting for transfers between devices  591 us (55%)
  other arithmetic  175 us (16%)
  local copies, waits for them, and re-layouts  93.2 us (9%)
  matrix products  90.5 us (8%)
  Pallas kernels  77.7 us (7%)
  starting transfers between devices  28.1 us (3%)
  between operations  15.5 us (1%)
    reduce_scatter x2, waiting for transfers between devices, reduce_rows(): stacked = lax.psum_scatter(stacked, OUTER, scatter_dimension=0, tiled=True)  246 us
    all_gather x2, waiting for transfers between devices, reduce_rows(): stacked = lax.all_gather(stacked, OUTER, axis=0, tiled=True)  136 us
    all_gather x2, waiting for transfers between devices, gather_rows(): got = lax.all_gather(other, OUTER, axis=0, tiled=False)  90.5 us
    add x5, other arithmetic, nesterov(): average_new = AVERAGING * average_old + (1.0 - AVERAGING) * weight_new  59.5 us
    pallas_call x4, Pallas kernels, group_attention_bwd(): pl.pallas_call(functools.partial(pair_bwd_kernel, score_scale), grid_spec...  45.3 us
    reduce_scatter x2, waiting for transfers between devices, reduce_rows(): stacked = lax.psum_scatter(stacked, SHARD, scatter_dimension=0, tiled=True)  39.5 us
    ppermute x8, waiting for transfers between devices, passed_along(): lax.ppermute(value, axis, [(source, source + steps) for source in range(l...  37.6 us
    select_n x4, other arithmetic, gather_ring(): jnp.where(first, jnp.concatenate([held, received], 0), jnp.concatenate([r...  33.4 us
  transfers between devices with their start and end apart: 24, of which 14 were waited for; matrix products, arithmetic and copies ran while one was open for 12% of the time, Pallas kernels for 6%

profile of v1, /device:TPU:9, one launch (start us, length us, event | category | flops | bytes accessed | tf_op | source)
XLA Modules:
  0.0 1071.0 jit_solution(15516937673508378152)
XLA Ops:
  40.9 12.3 %collective-permute-done.6 = bf16[288,1024]{1,0:T(8,128)(2,1)S(1)} collective-permute-done((bf16[288,1024]{1,0:T(8,128)(2,1)S(1)}, bf16[288,1024]{1,0:T(8,128)(2,1)S(1)}, u32[]{:S(2)}, u32[]{:S(2)}) %collective-permute-start.6) | collective-permute-done | bytes 589856 | tf_op jit(solution)/shard_map/ppermute | solution.py:211
  54.0 16.8 %all-gather.16.cloned.1.call-done = bf16[8,33,3072]{2,1,0:T(8,128)(2,1)} async-done(((bf16[1,33,3072]{2,1,0:T(8,128)(2,1)}), bf16[8,33,3072]{2,1,0:T(8,128)(2,1)}) %all-gather.16.cloned.1.call-update) | async-done | bytes 1622032 | tf_op jit(solution)/shard_map/all_gather | solution.py:212
  76.4 73.7 %all-gather.10.cloned.1.call-done = bf16[2304,1024]{1,0:T(8,128)(2,1)} async-done(((bf16[288,1024]{1,0:T(8,128)(2,1)}), bf16[2304,1024]{1,0:T(8,128)(2,1)}) %all-gather.10.cloned.1.call-update) | async-done | bytes 4718608 | tf_op jit(solution)/shard_map/all_gather | solution.py:212
  185.1 21.2 %collective-permute-done.5.kr_ref.vr_ref = bf16[512,512]{1,0:T(8,128)(2,1)} collective-permute-done((bf16[512,512]{1,0:T(8,128)(2,1)}, bf16[512,512]{1,0:T(8,128)(2,1)}, u32[]{:S(2)}, u32[]{:S(2)}) %collective-permute-start.5) | collective-permute-done | bytes 524320 | tf_op jit(solution)/shard_map/ppermute | solution.py:175
  281.1 13.4 %fusion.37 = bf16[4096,1024]{1,0:T(8,128)(2,1)} fusion(f32[512,1024]{1,0:T(8,128)S(1)} %copy-done.36, f32[512]{0:T(512)S(1)} %fusion.32, f32[512,4096]{1,0:T(8,128)} %fusion.39, f32[4096]{0:T(1024)S(1)} %bitcast.159), kind=kOutput, calls=%fused_computation.156 | convolution fusion | flops 4316987392 | bytes 18892800 | tf_op jit(solution)/shard_map/dot_general | solution.py:313
  294.5 14.2 %fusion.53 = (bf16[4096]{0:T(1024)(128)(2,1)S(1)}, bf16[512,4096]{1,0:T(8,128)(2,1)S(1)}) fusion(f32[512,4096]{1,0:T(8,128)} %fusion.39, f32[4096]{0:T(1024)S(1)} %bitcast.160, bf16[4096,1024]{1,0:T(8,128)(2,1)} %bitcast.130, f32[512,1024]{1,0:T(8,128)} %param.19, f32[512]{0:T(512)S(1)} %fusion.32), kind=kOutput, calls=%fused_computation.168 | convolution fusion | flops 4342149120 | bytes 23095296 | tf_op jit(solution)/shard_map/dot_general | solution.py:319
  333.3 11.4 %shard_map.312 = (f32[512,256]{1,0:T(8,128)S(1)}, f32[512,256]{1,0:T(8,128)S(1)}, f32[512,256]{1,0:T(8,128)S(1)}, f32[512,256]{1,0:T(8,128)S(1)}, f32[512,256]{1,0:T(8,128)S(1)}) custom-call(s32[2]{0:T(128)S(1)} %pad_add_fusion.info_ref, f32[4,1,128]{2,1,0:T(1,128)S(1)} %broadcast_in_dim.28.slope_ref, bf16[512,1024]{1,0:T(8,128)(2,1)S(1)} %get-tuple-element.123.q_ref, ...), custom_call_target="tpu_custom_call" | custom-call | flops 1073741824 | bytes 5242880 | tf_op jit(solution)/shard_map/pallas_call | solution.py:145
  347.1 11.3 %shard_map.311 = (f32[512,256]{1,0:T(8,128)S(1)}, f32[512,256]{1,0:T(8,128)S(1)}, f32[512,256]{1,0:T(8,128)S(1)}, f32[512,256]{1,0:T(8,128)S(1)}, f32[512,256]{1,0:T(8,128)S(1)}) custom-call(s32[2]{0:T(128)S(1)} %pad_add_fusion.info_ref, f32[4,1,128]{2,1,0:T(1,128)S(1)} %broadcast_in_dim.27.slope_ref, bf16[512,1024]{1,0:T(8,128)(2,1)S(1)} %get-tuple-element.123.q_ref, ...), custom_call_target="tpu_custom_call" | custom-call | flops 1073741824 | bytes 5242880 | tf_op jit(solution)/shard_map/pallas_call | solution.py:145
  360.7 11.4 %shard_map.310 = (f32[512,256]{1,0:T(8,128)S(1)}, f32[512,256]{1,0:T(8,128)S(1)}, f32[512,256]{1,0:T(8,128)S(1)}, f32[512,256]{1,0:T(8,128)S(1)}, f32[512,256]{1,0:T(8,128)S(1)}) custom-call(s32[2]{0:T(128)S(1)} %pad_add_fusion.info_ref, f32[4,1,128]{2,1,0:T(1,128)S(1)} %broadcast_in_dim.26.slope_ref, bf16[512,1024]{1,0:T(8,128)(2,1)S(1)} %get-tuple-element.123.q_ref, ...), custom_call_target="tpu_custom_call" | custom-call | flops 1073741824 | bytes 5242880 | tf_op jit(solution)/shard_map/pallas_call | solution.py:145
  373.0 11.2 %shard_map.309 = (f32[512,256]{1,0:T(8,128)S(1)}, f32[512,256]{1,0:T(8,128)S(1)}, f32[512,256]{1,0:T(8,128)S(1)}, f32[512,256]{1,0:T(8,128)S(1)}, f32[512,256]{1,0:T(8,128)S(1)}) custom-call(s32[2]{0:T(128)S(1)} %pad_add_fusion.info_ref, f32[4,1,128]{2,1,0:T(1,128)S(1)} %broadcast_in_dim.24.slope_ref, bf16[512,1024]{1,0:T(8,128)(2,1)S(1)} %get-tuple-element.123.q_ref, ...), custom_call_target="tpu_custom_call" | custom-call | flops 1073741824 | bytes 5242880 | tf_op jit(solution)/shard_map/pallas_call | solution.py:145
  436.5 11.9 %copy.102 = bf16[2,2,8,32,3072]{4,1,3,0,2:T(2,128)(2,1)S(1)} copy(bf16[2,2,8,32,3072]{4,3,2,1,0:T(8,128)(2,1)} %bitcast.136) | data formatting | bytes 12582912 | tf_op jit(solution)/shard_map/convert_element_type | solution.py:237
  463.7 15.8 %pad_maximum_fusion = bf16[2,8,2,288,1024]{4,3,2,1,0:T(8,128)(2,1)} fusion(bf16[2,8,2,128,1024]{4,3,2,1,0:T(8,128)(2,1)} %bitcast.132, bf16[2,8,2,128,1024]{4,3,2,1,0:T(8,128)(2,1)} %bitcast.133, bf16[2,8,2,32,1024]{4,3,2,1,0:T(8,128)(2,1)S(1)} %bitcast.129), kind=kLoop, calls=%fused_computation | loop fusion | flops 56623104 | bytes 37748736 | tf_op jit(solution)/shard_map/concatenate | solution.py:237
  483.3 23.9 %reduce-scatter.13.cloned.1.call-done = bf16[1,4608,1024]{2,1,0:T(8,128)(2,1)} async-done(((bf16[2,4608,1024]{2,1,0:T(8,128)(2,1)}), bf16[1,4608,1024]{2,1,0:T(8,128)(2,1)}) %reduce-scatter.13.cloned.1.call-update) | async-done | bytes 9437200 | tf_op jit(solution)/shard_map/reduce_scatter | solution.py:239
  507.2 83.4 %reduce-scatter.9.cloned.1.call-done = bf16[1,66,3072]{2,1,0:T(8,128)(2,1)} async-done(((bf16[8,66,3072]{2,1,0:T(8,128)(2,1)}), bf16[1,66,3072]{2,1,0:T(8,128)(2,1)}) %reduce-scatter.9.cloned.1.call-update) | async-done | bytes 405520 | tf_op jit(solution)/shard_map/reduce_scatter | solution.py:241
  592.6 162.4 %reduce-scatter.15.cloned.1.call-done = bf16[1,576,1024]{2,1,0:T(8,128)(2,1)} async-done(((bf16[8,576,1024]{2,1,0:T(8,128)(2,1)}), bf16[1,576,1024]{2,1,0:T(8,128)(2,1)}) %reduce-scatter.15.cloned.1.call-update) | async-done | bytes 1179664 | tf_op jit(solution)/shard_map/reduce_scatter | solution.py:241
  755.0 17.5 %reduce-scatter.11.cloned.1.call-done = bf16[1,33,3072]{2,1,0:T(8,128)(2,1)} async-done(((bf16[2,33,3072]{2,1,0:T(8,128)(2,1)}), bf16[1,33,3072]{2,1,0:T(8,128)(2,1)}) %reduce-scatter.11.cloned.1.call-update) | async-done | bytes 202768 | tf_op jit(solution)/shard_map/reduce_scatter | solution.py:243
  774.6 22.0 %reduce-scatter.17.cloned.1.call-done = bf16[1,288,1024]{2,1,0:T(8,128)(2,1)} async-done(((bf16[2,288,1024]{2,1,0:T(8,128)(2,1)}), bf16[1,288,1024]{2,1,0:T(8,128)(2,1)}) %reduce-scatter.17.cloned.1.call-update) | async-done | bytes 589840 | tf_op jit(solution)/shard_map/reduce_scatter | solution.py:243
  796.6 62.5 %all-gather.12.cloned.1.call-done = bf16[1,264,3072]{2,0,1:T(2,128)(2,1)} async-done(((bf16[1,33,3072]{2,0,1:T(2,128)(2,1)}), bf16[1,264,3072]{2,0,1:T(2,128)(2,1)}) %all-gather.12.cloned.1.call-update) | async-done | bytes 1622032 | tf_op jit(solution)/shard_map/all_gather | solution.py:245
  864.9 73.4 %all-gather.14.cloned.1.call-done = bf16[1,2304,1024]{2,1,0:T(8,128)(2,1)} async-done(((bf16[1,288,1024]{2,1,0:T(8,128)(2,1)}), bf16[1,2304,1024]{2,1,0:T(8,128)(2,1)}) %all-gather.14.cloned.1.call-update) | async-done | bytes 4718608 | tf_op jit(solution)/shard_map/all_gather | solution.py:245
  940.8 12.5 %add_add_fusion = f32[512,1024]{1,0:T(8,128)} fusion(f32[512,1024]{1,0:T(8,128)S(1)} %copy-done.31, bf16[4096,1024]{1,0:T(8,128)(2,1)} %bitcast.131, f32[1024]{0:T(1024)S(1)} %bitcast.163, f32[512,4096]{1,0:T(8,128)} %fusion.39, f32[4096]{0:T(1024)S(1)} %bitcast.161), kind=kOutput, calls=%fused_computation.62 | convolution fusion | flops 4316987392 | bytes 20992000 | tf_op jit(solution)/shard_map/dot_general | solution.py:443
  957.5 14.2 %broadcast_select_fusion = bf16[2,264,3072]{2,0,1:T(2,128)(2,1)S(1)} fusion(pred[]{:T(512)S(6)} %eq.7, bf16[1,264,3072]{2,0,1:T(2,128)(2,1)S(1)} %copy.93, bf16[1,264,3072]{2,0,1:T(2,128)(2,1)S(1)} %copy-done.26), kind=kLoop, calls=%fused_computation.27 | loop fusion | flops 14598144 | bytes 6488065 | tf_op jit(solution)/shard_map/jit(_where)/select_n | solution.py:195
  978.9 12.1 %multiply_add_fusion.2 = (f32[512,3072]{1,0:T(8,128)}, f32[512,3072]{1,0:T(8,128)}, f32[512,3072]{1,0:T(8,128)}) fusion(f32[512,3072]{1,0:T(8,128)} %param.23, f32[512,3072]{1,0:T(8,128)} %param.21, bf16[16,32,3072]{2,1,0:T(8,128)(2,1)S(1)} %slice.239, f32[512,3072]{1,0:T(8,128)} %param.22), kind=kLoop, calls=%fused_computation.32 | loop fusion | flops 15728640 | bytes 40894464 | tf_op jit(solution)/shard_map/add | solution.py:336
  1023.0 22.3 %multiply_add_fusion.1 = (f32[1024,2048]{1,0:T(8,128)}, f32[1024,2048]{1,0:T(8,128)}, f32[1024,2048]{1,0:T(8,128)}) fusion(f32[1024,2048]{1,0:T(8,128)} %param.29, f32[1024,2048]{1,0:T(8,128)} %param.27, f32[2048,1024]{0,1:T(8,128)} %copy.98, f32[1024,2048]{1,0:T(8,128)} %param.28), kind=kLoop, calls=%fused_computation.22 | loop fusion | flops 18874368 | bytes 58720256 | tf_op jit(solution)/shard_map/add | solution.py:336
  1045.3 18.6 %multiply_add_fusion = (f32[2048,1024]{1,0:T(8,128)}, f32[2048,1024]{1,0:T(8,128)}, f32[2048,1024]{1,0:T(8,128)}) fusion(f32[2048,1024]{1,0:T(8,128)} %param.32, f32[2048,1024]{1,0:T(8,128)} %param.30, bf16[16,128,1024]{2,1,0:T(8,128)(2,1)} %get-tuple-element.118, f32[2048,1024]{1,0:T(8,128)} %param.31), kind=kLoop, calls=%fused_computation.21 | loop fusion | flops 20971520 | bytes 54525952 | tf_op jit(solution)/shard_map/add | solution.py:336
  (313 shorter events, 305.8 us)
Async XLA Ops:
  7.2 63.7 %all-gather.16.cloned.1.call-start = ((), (), s32[]{:S(2)}) async-start(), calls=%async_computation.15 | async-start | bytes 2211840 | tf_op jit(solution)/shard_map/all_gather | solution.py:212
  14.2 6.9 collective-permute-start
  21.8 128.3 %all-gather.10.cloned.1.call-start = ((), (), s32[]{:S(2)}) async-start(), calls=%async_computation.12 | async-start | bytes 5308416 | tf_op jit(solution)/shard_map/all_gather | solution.py:212
  39.6 13.6 %collective-permute-start.6 = (bf16[288,1024]{1,0:T(8,128)(2,1)S(1)}, bf16[288,1024]{1,0:T(8,128)(2,1)S(1)}, u32[]{:S(2)}, u32[]{:S(2)}) collective-permute-start(bf16[288,1024]{1,0:T(8,128)(2,1)S(1)} %pad_maximum_fusion.2), channel_id=1, source_target_pairs={{0,1},{1,0},{2,3},{3,2},{4,5},{5,4},{6,7},{7,6},{8,9},{9,8},{10,11... | collective-permute-start | bytes 1769480 | tf_op jit(solution)/shard_map/ppermute | solution.py:211
  54.0 425.5 %reduce-scatter.7.cloned.1.call-start = ((), (), s32[]{:S(2)}) async-start(), calls=%async_computation.6 | async-start | bytes 9732096 | tf_op jit(solution)/shard_map/reduce_scatter | solution.py:239
  74.5 79.1 %collective-permute-start.1 = (bf16[1,8,33,3072]{3,1,2,0:T(8,128)(2,1)}, bf16[1,8,33,3072]{3,1,2,0:T(8,128)(2,1)}, u32[]{:S(2)}, u32[]{:S(2)}) collective-permute-start(bf16[1,8,33,3072]{3,1,2,0:T(8,128)(2,1)} %copy.78), channel_id=1, source_target_pairs={{0,2},{2,0},{1,3},{3,1},{4,6},{6,4},{5,7},{7,5},{8,10},{10,8},{9,1... | collective-permute-start | bytes 4866056 | tf_op jit(solution)/shard_map/ppermute | solution.py:193
  150.1 93.2 %collective-permute-start.7 = (bf16[1,8,288,1024]{3,2,1,0:T(8,128)(2,1)}, bf16[1,8,288,1024]{3,2,1,0:T(8,128)(2,1)}, u32[]{:S(2)}, u32[]{:S(2)}) collective-permute-start(bf16[1,8,288,1024]{3,2,1,0:T(8,128)(2,1)} %bitcast.137), channel_id=1, source_target_pairs={{0,2},{2,0},{1,3},{3,1},{4,6},{6,4},{5,7},{7,5},{8,10},{10,8},{9,1... | collective-permute-start | bytes 14155784 | tf_op jit(solution)/shard_map/ppermute | solution.py:193
  169.2 64.5 %collective-permute-start.2 = (bf16[512,512]{1,0:T(8,128)(2,1)}, bf16[512,512]{1,0:T(8,128)(2,1)}, u32[]{:S(2)}, u32[]{:S(2)}) collective-permute-start(bf16[512,512]{1,0:T(8,128)(2,1)} %pad_maximum_fusion.3), channel_id=1, source_target_pairs={{0,1},{2,3},{4,5},{6,7},{8,9},{10,11},{12,13},{14,15},{16,17},{18,... | collective-permute-start | bytes 1572872 | tf_op jit(solution)/shard_map/ppermute | solution.py:175
  173.9 41.5 %collective-permute-start.4 = (bf16[512,512]{1,0:T(8,128)(2,1)}, bf16[512,512]{1,0:T(8,128)(2,1)}, u32[]{:S(2)}, u32[]{:S(2)}) collective-permute-start(bf16[512,512]{1,0:T(8,128)(2,1)} %pad_maximum_fusion.5), channel_id=1, source_target_pairs={{0,1},{2,3},{4,5},{6,7},{8,9},{10,11},{12,13},{14,15},{16,17},{18,... | collective-permute-start | bytes 1572872 | tf_op jit(solution)/shard_map/ppermute | solution.py:175
  176.8 29.5 %collective-permute-start.5 = (bf16[512,512]{1,0:T(8,128)(2,1)}, bf16[512,512]{1,0:T(8,128)(2,1)}, u32[]{:S(2)}, u32[]{:S(2)}) collective-permute-start(bf16[512,512]{1,0:T(8,128)(2,1)} %pad_maximum_fusion.6), channel_id=1, source_target_pairs={{0,1},{2,3},{4,5},{6,7},{8,9},{10,11},{12,13},{14,15},{16,17},{18,... | collective-permute-start | bytes 1572872 | tf_op jit(solution)/shard_map/ppermute | solution.py:175
  179.8 44.8 %collective-permute-start.3 = (bf16[512,512]{1,0:T(8,128)(2,1)}, bf16[512,512]{1,0:T(8,128)(2,1)}, u32[]{:S(2)}, u32[]{:S(2)}) collective-permute-start(bf16[512,512]{1,0:T(8,128)(2,1)} %pad_maximum_fusion.4), channel_id=1, source_target_pairs={{0,1},{2,3},{4,5},{6,7},{8,9},{10,11},{12,13},{14,15},{16,17},{18,... | collective-permute-start | bytes 1572872 | tf_op jit(solution)/shard_map/ppermute | solution.py:175
  345.8 68.4 %collective-permute-start.11 = (bf16[512,512]{1,0:T(8,128)(2,1)}, bf16[512,512]{1,0:T(8,128)(2,1)S(1)}, u32[]{:S(2)}, u32[]{:S(2)}) collective-permute-start(bf16[512,512]{1,0:T(8,128)(2,1)} %pad_maximum_fusion.10), channel_id=1, source_target_pairs={{1,0},{3,2},{5,4},{7,6},{9,8},{11,10},{13,12},{15,14},{17,16},{19,... | collective-permute-start | bytes 1572872 | tf_op jit(solution)/shard_map/ppermute | solution.py:175
  359.4 43.8 %collective-permute-start.10 = (bf16[512,512]{1,0:T(8,128)(2,1)}, bf16[512,512]{1,0:T(8,128)(2,1)}, u32[]{:S(2)}, u32[]{:S(2)}) collective-permute-start(bf16[512,512]{1,0:T(8,128)(2,1)} %pad_maximum_fusion.9), channel_id=1, source_target_pairs={{1,0},{3,2},{5,4},{7,6},{9,8},{11,10},{13,12},{15,14},{17,16},{19,... | collective-permute-start | bytes 1572872 | tf_op jit(solution)/shard_map/ppermute | solution.py:175
  385.9 15.3 %collective-permute-start.8 = (bf16[512,512]{1,0:T(8,128)(2,1)}, bf16[512,512]{1,0:T(8,128)(2,1)S(1)}, u32[]{:S(2)}, u32[]{:S(2)}) collective-permute-start(bf16[512,512]{1,0:T(8,128)(2,1)} %pad_maximum_fusion.7), channel_id=1, source_target_pairs={{1,0},{3,2},{5,4},{7,6},{9,8},{11,10},{13,12},{15,14},{17,16},{19,... | collective-permute-start | bytes 1572872 | tf_op jit(solution)/shard_map/ppermute | solution.py:175
  388.0 24.4 %collective-permute-start.9 = (bf16[512,512]{1,0:T(8,128)(2,1)}, bf16[512,512]{1,0:T(8,128)(2,1)S(1)}, u32[]{:S(2)}, u32[]{:S(2)}) collective-permute-start(bf16[512,512]{1,0:T(8,128)(2,1)} %pad_maximum_fusion.8), channel_id=1, source_target_pairs={{1,0},{3,2},{5,4},{7,6},{9,8},{11,10},{13,12},{15,14},{17,16},{19,... | collective-permute-start | bytes 1572872 | tf_op jit(solution)/shard_map/ppermute | solution.py:175
  461.8 45.4 %reduce-scatter.13.cloned.1.call-start = ((), (), s32[]{:S(2)}) async-start(), calls=%async_computation.9 | async-start | bytes 28311552 | tf_op jit(solution)/shard_map/reduce_scatter | solution.py:239
  479.5 111.1 %reduce-scatter.9.cloned.1.call-start = ((), (), s32[]{:S(2)}) async-start(), calls=%async_computation.7 | async-start | bytes 3981312 | tf_op jit(solution)/shard_map/reduce_scatter | solution.py:241
  483.2 271.7 %reduce-scatter.15.cloned.1.call-start = ((), (), s32[]{:S(2)}) async-start(), calls=%async_computation.10 | async-start | bytes 10616832 | tf_op jit(solution)/shard_map/reduce_scatter | solution.py:241
  507.2 265.3 %reduce-scatter.11.cloned.1.call-start = ((), (), s32[]{:S(2)}) async-start(), calls=%async_computation.8 | async-start | bytes 737280 | tf_op jit(solution)/shard_map/reduce_scatter | solution.py:243
  592.5 204.1 %reduce-scatter.17.cloned.1.call-start = ((), (), s32[]{:S(2)}) async-start(), calls=%async_computation.11 | async-start | bytes 1769472 | tf_op jit(solution)/shard_map/reduce_scatter | solution.py:243
  755.0 104.1 %all-gather.12.cloned.1.call-start = ((), (), s32[]{:S(2)}) async-start(), calls=%async_computation.13 | async-start | bytes 3649536 | tf_op jit(solution)/shard_map/all_gather | solution.py:245
  774.5 163.8 %all-gather.14.cloned.1.call-start = ((), (), s32[]{:S(2)}) async-start(), calls=%async_computation.14 | async-start | bytes 5308416 | tf_op jit(solution)/shard_map/all_gather | solution.py:245
  862.7 90.7 %collective-permute-start.12 = (bf16[1,264,3072]{2,1,0:T(8,128)(2,1)}, bf16[1,264,3072]{2,1,0:T(8,128)(2,1)}, u32[]{:S(2)}, u32[]{:S(2)}) collective-permute-start(bf16[1,264,3072]{2,1,0:T(8,128)(2,1)} %copy.92), channel_id=1, source_target_pairs={{0,2},{2,0},{1,3},{3,1},{4,6},{6,4},{5,7},{7,5},{8,10},{10,8},{9,1... | collective-permute-start | bytes 4866056 | tf_op jit(solution)/shard_map/ppermute | solution.py:193
  938.3 52.7 %collective-permute-start.13 = (bf16[1,2304,1024]{2,1,0:T(8,128)(2,1)}, bf16[1,2304,1024]{2,1,0:T(8,128)(2,1)}, u32[]{:S(2)}, u32[]{:S(2)}) collective-permute-start(bf16[1,2304,1024]{2,1,0:T(8,128)(2,1)} %all-gather.14.cloned.1.call-done), channel_id=1, source_target_pairs={{0,2},{2,0},{1,3},{3,1},{4,6},{6,4},{5,7},{7,5},{8,10},{10,8},{9,1... | collective-permute-start | bytes 14155784 | tf_op jit(solution)/shard_map/ppermute | solution.py:193
  (54 other events, 1227.9 us)
Sparse Core Ops, SparseCore 0:
  21.9 48.8 all-gather.15
  73.6 76.4 all-gather.9
  461.9 14.3 reduce-scatter.6
  479.6 27.5 reduce-scatter.12
  511.2 79.3 reduce-scatter.8
  594.1 160.8 reduce-scatter.14
  757.8 14.6 reduce-scatter.10
  774.8 21.8 reduce-scatter.16
  799.4 59.7 all-gather.11
  861.1 77.1 all-gather.13
